TPU v7x, 32 devices: a whole 2x2x4 slice. The times are simulated.
32 devices in a mesh: row: 4 (over z), col: 8 (over y, x, core).
Axes of the slice: x: 2, y: 2, z: 4, core: 2. Of those that a mesh axis runs over, the one named last changes fastest.
Arguments:
- pencil_a: float32 [4, 3072, 8, 1536], P('row', None, 'col'), may hold values from -6 to 6, as said below
- pencil_b: float32 [4, 3072, 8, 1536], P('row', None, 'col'), may hold values from -6 to 6
Outputs:
- new_a: float32 [4, 3072, 8, 1536], P('row', None, 'col')
- new_b: float32 [4, 3072, 8, 1536], P('row', None, 'col')
Inputs may be any that keep to these rules, and one draw needn't show every extreme that they name: `pencil_a`: the first 256 columns of Amat are zero in the last 256 rows of Amat.
All inputs are finite; a program needn't handle non-finite values.
Results may differ from a plain program's by a relative error of at most 0.000056.
Values sent between devices are 32-bit elements; how exact they have to be, the bound alone decides.
A program may use at most 192 MiB of HBM per device.

v0:
```python
import jax
import jax.numpy as jnp
from jax import lax
from jax.sharding import PartitionSpec as P

NB = 256


def broadcast(array, axis, root):
    mine = lax.axis_index(axis) == root
    return lax.psum(jnp.where(mine, array, jnp.zeros_like(array)), axis)


def matmul(left, right):
    return jnp.dot(left, right, precision=lax.Precision.HIGHEST, preferred_element_type=jnp.float32)


def inverse_factor(gram):
    lower = jnp.linalg.cholesky(gram)
    ident = jnp.eye(gram.shape[0], dtype=jnp.float32)
    return jax.scipy.linalg.solve_triangular(lower, ident, lower=True).T


def general_inverse(square):
    lower = jnp.linalg.cholesky(matmul(square, square.T))
    ident = jnp.eye(square.shape[0], dtype=jnp.float32)
    linv = jax.scipy.linalg.solve_triangular(lower, ident, lower=True)
    return matmul(square.T, matmul(linv.T, linv))


def fast_matmul(left, right):
    return jnp.dot(left, right, precision=lax.Precision.HIGH, preferred_element_type=jnp.float32)


def on_device(pencil_a, pencil_b):
    rows_loc = pencil_a.shape[1]
    cols_loc = pencil_a.shape[3]
    amat = pencil_a.reshape(rows_loc, cols_loc)
    bmat = pencil_b.reshape(rows_loc, cols_loc)
    width = NB
    ident = jnp.eye(width, dtype=jnp.float32)
    row = lax.axis_index("row")
    col = lax.axis_index("col")
    last_row = lax.axis_size("row") - 1
    last_col = lax.axis_size("col") - 1
    top_mask = (row == 0).astype(jnp.float32)
    end_mask = (col == last_col).astype(jnp.float32)
    own_panel = amat[:, :width]
    own_strip = bmat[rows_loc - width :]
    zero = jnp.zeros((width, width), jnp.float32)
    small = jnp.stack(
        [
            jnp.where(col == 0, matmul(own_panel.T, own_panel), zero),
            jnp.where((col == 0) & (row == 0), own_panel[:width], zero),
            jnp.where(row == last_row, matmul(own_strip, own_strip.T), zero),
            jnp.where(
                (col == last_col) & (row == last_row), own_strip[:, cols_loc - width :], zero
            ),
        ]
    )
    small = lax.psum(small, ("row", "col"))
    own_panel, own_strip, small = lax.optimization_barrier((own_panel, own_strip, small))
    panel = broadcast(own_panel, "col", 0)
    strip = broadcast(own_strip, "row", last_row)
    left_inv = inverse_factor(small[0])
    right_inv = inverse_factor(small[2])
    vectors = matmul(panel, left_inv) + top_mask * jnp.pad(ident, ((0, rows_loc - width), (0, 0)))
    vectors_t = matmul(right_inv.T, strip) + end_mask * jnp.pad(
        ident, ((0, 0), (cols_loc - width, 0))
    )
    vectors, strip = lax.optimization_barrier((vectors, strip))
    products_a, products_b = lax.psum(
        (fast_matmul(vectors.T, amat), fast_matmul(vectors.T, bmat)), "row"
    )
    share = lax.psum_scatter(
        jnp.concatenate([fast_matmul(amat, vectors_t.T), fast_matmul(bmat, vectors_t.T)], axis=1),
        "col",
        scatter_dimension=0,
        tiled=True,
    )
    kinv_right = general_inverse(ident + matmul(right_inv.T, small[3]).T)
    kinv_left = general_inverse(ident + matmul(small[1], left_inv))
    scaled = jnp.concatenate(
        [matmul(share[:, :width], kinv_right.T), matmul(share[:, width:], kinv_right.T)], axis=1
    )
    gathered = lax.all_gather(scaled, "col", axis=0, tiled=True)
    cross = lax.psum(
        jnp.concatenate([matmul(products_a, vectors_t.T), matmul(products_b, vectors_t.T)], axis=0),
        "col",
    )

    def update(matrix, products, mixed, crossed):
        inner = products - matmul(matmul(crossed, kinv_right.T), vectors_t)
        low = jnp.concatenate([matmul(kinv_left, inner), vectors_t], axis=0)
        return matrix - fast_matmul(jnp.concatenate([vectors, mixed], axis=1), low)

    amat = update(amat, products_a, gathered[:, :width], cross[:width])
    bmat = update(bmat, products_b, gathered[:, width:], cross[width:])
    return (amat.reshape(1, rows_loc, 1, cols_loc), bmat.reshape(1, rows_loc, 1, cols_loc))


def solution(mesh):
    placed = (P("row", None, "col", None), P("row", None, "col", None))
    return jax.shard_map(
        on_device,
        mesh=mesh,
        in_specs=placed,
        out_specs=(P("row", None, "col", None), P("row", None, "col", None)),
        check_vma=False,
    )
```

profile of v0, /device:TPU:0, one launch (start us, length us, event | category | flops | bytes accessed | tf_op | source)
XLA Modules:
  0.0 798.0 jit_solution(4191456055535194326)
XLA Ops:
  12.6 39.6 %copy.4 = f32[1,3072,1,1536]{1,3,2,0:T(8,128)} copy(f32[1,3072,1,1536]{3,2,1,0:T(1,128)} %param.5) | data formatting | bytes 37748736 | tf_op args[0]
  63.9 129.5 %all-reduce.10.cloned.1.call-done = f32[4,256,256]{1,2,0:T(8,128)} async-done(((f32[4,256,256]{1,2,0:T(8,128)}), f32[4,256,256]{1,2,0:T(8,128)}) %all-reduce.10.cloned.1.call-update) | async-done | bytes 1048592 | tf_op jit(solution)/shard_map/psum | solution.py:61
  201.9 11.7 %cholesky.248 = f32[128,128]{1,0:T(8,128)S(1)} custom-call(f32[128,128]{1,0:T(8,128)S(1)} %cholesky.349), custom_call_target="Cholesky" | custom-call | tf_op jit(solution)/shard_map/jit(cholesky)/cholesky | solution.py:19
  249.6 11.7 %cholesky.265 = f32[128,128]{1,0:T(8,128)S(1)} custom-call(f32[128,128]{1,0:T(8,128)S(1)} %convolution_subtract_fusion.8), custom_call_target="Cholesky" | custom-call | tf_op jit(solution)/shard_map/jit(cholesky)/cholesky | solution.py:19
  264.2 11.7 %cholesky.231 = f32[128,128]{1,0:T(8,128)S(1)} custom-call(f32[128,128]{1,0:T(8,128)S(1)} %convolution_subtract_fusion.9), custom_call_target="Cholesky" | custom-call | tf_op jit(solution)/shard_map/jit(cholesky)/cholesky | solution.py:19
  288.8 19.7 %custom-call.20 = f32[2,128,128]{1,2,0:T(8,128)S(1)} custom-call(f32[2,128,128]{2,1,0:T(8,128)S(1)} %get-tuple-element.39), custom_call_target="InvertDiagBlocksLowerTriangular" | custom-call | tf_op jit(solution)/shard_map/jit(_solve_triangular)/triangular_solve | solution.py:21
  308.5 19.7 %custom-call.18 = f32[2,128,128]{1,2,0:T(8,128)S(1)} custom-call(f32[2,128,128]{2,1,0:T(8,128)S(1)} %get-tuple-element.38), custom_call_target="InvertDiagBlocksLowerTriangular" | custom-call | tf_op jit(solution)/shard_map/jit(_solve_triangular)/triangular_solve | solution.py:21
  337.7 14.5 %all-reduce.14.cloned.1.call-done = f32[256,1536]{0,1:T(8,128)} async-done(((f32[256,1536]{0,1:T(8,128)}), f32[256,1536]{0,1:T(8,128)}) %all-reduce.14.cloned.1.call-update) | async-done | bytes 1572880 | tf_op jit(solution)/shard_map/psum | solution.py:11
  352.2 17.5 %fusion = f32[256,1536]{1,0:T(8,128)} fusion(f32[3072,256]{1,0:T(8,128)S(1)} %convolution_add_fusion, f32[1,3072,1,1536]{3,2,1,0:T(1,128)} %param.6), kind=kOutput, calls=%fused_computation.9 | convolution fusion | flops 7247757312 | bytes 23592960 | tf_op jit(solution)/shard_map/dot_general | solution.py:32
  369.6 19.3 %fusion.80 = f32[256,1536]{1,0:T(8,128)} fusion(f32[3072,256]{1,0:T(8,128)S(1)} %convolution_add_fusion, f32[1,3072,1,1536]{1,3,2,0:T(8,128)} %copy.4), kind=kOutput, calls=%fused_computation.170 | convolution fusion | flops 7247757312 | bytes 23592960 | tf_op jit(solution)/shard_map/dot_general | solution.py:32
  394.2 15.4 %fusion.9 = f32[3072,256]{0,1:T(8,128)S(1)} fusion(f32[256,1536]{1,0:T(8,128)S(1)} %convolution_add_fusion.1, f32[1,3072,1,1536]{3,2,1,0:T(1,128)} %param.6), kind=kOutput, calls=%fused_computation.22 | convolution fusion | flops 7247757312 | bytes 23592960 | tf_op jit(solution)/shard_map/dot_general | solution.py:32
  409.6 11.9 %convolution_bitcast_fusion = f32[3072,256]{0,1:T(8,128)S(1)} fusion(f32[256,1536]{1,0:T(8,128)S(1)} %convolution_add_fusion.1, f32[1,3072,1,1536]{1,3,2,0:T(8,128)} %copy.4), kind=kOutput, calls=%fused_computation.23 | convolution fusion | flops 7247757312 | bytes 23592960 | tf_op jit(solution)/shard_map/dot_general | solution.py:32
  429.2 11.7 %cholesky.282 = f32[128,128]{1,0:T(8,128)S(1)} custom-call(f32[128,128]{1,0:T(8,128)S(1)} %cholesky.352), custom_call_target="Cholesky" | custom-call | tf_op jit(solution)/shard_map/jit(cholesky)/cholesky | solution.py:25
  455.6 13.2 %cholesky.299 = f32[128,128]{1,0:T(8,128)} custom-call(f32[128,128]{1,0:T(8,128)} %convolution_subtract_fusion.7), custom_call_target="Cholesky" | custom-call | tf_op jit(solution)/shard_map/jit(cholesky)/cholesky | solution.py:25
  479.3 21.1 %custom-call.22 = f32[2,128,128]{1,2,0:T(8,128)} custom-call(f32[2,128,128]{2,1,0:T(8,128)} %get-tuple-element.40), custom_call_target="InvertDiagBlocksLowerTriangular" | custom-call | tf_op jit(solution)/shard_map/jit(_solve_triangular)/triangular_solve | solution.py:27
  514.7 58.9 %reduce-scatter.2.cloned.1.call-done = f32[384,512]{0,1:T(8,128)} async-done(((f32[3072,512]{0,1:T(8,128)}), f32[384,512]{0,1:T(8,128)}) %reduce-scatter.2.cloned.1.call-update) | async-done | bytes 786448 | tf_op jit(solution)/shard_map/reduce_scatter | solution.py:75
  580.4 11.7 %cholesky.316 = f32[128,128]{1,0:T(8,128)S(1)} custom-call(f32[128,128]{1,0:T(8,128)S(1)} %cholesky.355), custom_call_target="Cholesky" | custom-call | tf_op jit(solution)/shard_map/jit(cholesky)/cholesky | solution.py:25
  602.4 12.1 %cholesky.333 = f32[128,128]{1,0:T(8,128)S(1)} custom-call(f32[128,128]{1,0:T(8,128)S(1)} %convolution_subtract_fusion.6), custom_call_target="Cholesky" | custom-call | tf_op jit(solution)/shard_map/jit(cholesky)/cholesky | solution.py:25
  620.9 19.7 %custom-call.24 = f32[2,128,128]{1,2,0:T(8,128)S(1)} custom-call(f32[2,128,128]{2,1,0:T(8,128)S(1)} %get-tuple-element.41), custom_call_target="InvertDiagBlocksLowerTriangular" | custom-call | tf_op jit(solution)/shard_map/jit(_solve_triangular)/triangular_solve | solution.py:27
  654.2 24.6 %all-gather.2.cloned.1.call-done = f32[3072,512]{1,0:T(8,128)} async-done(((f32[384,512]{1,0:T(8,128)}), f32[3072,512]{1,0:T(8,128)}) %all-gather.2.cloned.1.call-update) | async-done | bytes 6291472 | tf_op jit(solution)/shard_map/all_gather | solution.py:86
  683.9 20.7 %subtract_bitcast_fusion = f32[1,3072,1,1536]{1,3,2,0:T(8,128)} fusion(f32[3072,256]{1,0:T(8,128)S(1)} %copy-done.1, f32[3072,256]{1,0:T(8,128)S(1)} %get-tuple-element.87, f32[256,1536]{1,0:T(8,128)S(1)} %convolution_add_fusion.1, f32[256,1536]{1,0:T(8,128)S(1)} %copy-done.2, f32[1,3072,1,1536]{1,3,2,0:T(8,128)} %copy.4), kind=kOutput, calls=%fused_computation.14 | convolution fusion | flops 14502592512 | bytes 47185920 | tf_op jit(solution)/shard_map/dot_general | solution.py:32
  704.5 39.7 %copy.15 = f32[1,3072,1,1536]{3,2,1,0:T(1,128)} copy(f32[1,3072,1,1536]{1,3,2,0:T(8,128)} %subtract_bitcast_fusion) | data formatting | bytes 37748736
  744.2 24.4 %fusion.4 = f32[1,3072,1,1536]{3,1,2,0:T(8,128)} fusion(f32[1,3072,1,1536]{3,2,1,0:T(1,128)} %param.6, f32[3072,256]{1,0:T(8,128)} %copy-done, f32[3072,256]{1,0:T(8,128)} %get-tuple-element.86, f32[256,1536]{1,0:T(8,128)S(1)} %convolution_add_fusion.1, f32[256,1536]{1,0:T(8,128)S(1)} %fusion.96), kind=kOutput, calls=%fused_computation.13 | convolution fusion | flops 14502592512 | bytes 47185920 | tf_op jit(solution)/shard_map/dot_general | solution.py:32
  768.6 22.3 %copy.16 = f32[1,3072,1,1536]{3,2,1,0:T(1,128)} copy(f32[1,3072,1,1536]{3,1,2,0:T(8,128)} %fusion.4) | data formatting | bytes 37748736
  (183 shorter events, 192.6 us)
Async XLA Ops:
  7.2 1.4 slice-start
  7.2 186.2 %all-reduce.10.cloned.1.call-start = ((), (), s32[]{:S(2)}) async-start(), calls=%async_computation.1 | async-start | bytes 2097152 | tf_op jit(solution)/shard_map/psum | solution.py:61
  59.9 270.8 %all-reduce.12.cloned.1.call-start = ((), (), s32[]{:S(2)}) async-start(), calls=%async_computation.2 | async-start | bytes 6291456 | tf_op jit(solution)/shard_map/psum | solution.py:11
  197.3 1.2 copy-start.7
  197.3 154.9 %all-reduce.14.cloned.1.call-start = ((), (), s32[]{:S(2)}) async-start(), calls=%async_computation.3 | async-start | bytes 3145728 | tf_op jit(solution)/shard_map/psum | solution.py:11
  284.4 46.3 %copy-start.11 = (f32[256,256]{1,0:T(8,128)}, f32[256,256]{1,0:T(8,128)S(1)}, u32[]{:S(2)}) copy-start(f32[256,256]{1,0:T(8,128)S(1)} %get-tuple-element.325) | copy-start | bytes 786436
  284.5 224.7 %all-reduce.18.cloned.1.call-start = ((), (), s32[]{:S(2)}) async-start(), calls=%async_computation.7 | async-start | bytes 6291456 | tf_op jit(solution)/shard_map/psum | solution.py:72
  308.5 20.7 %copy-start.16 = (f32[2,128,128]{1,2,0:T(8,128)}, f32[2,128,128]{1,2,0:T(8,128)S(1)}, u32[]{:S(2)}) copy-start(f32[2,128,128]{1,2,0:T(8,128)S(1)} %custom-call.20) | copy-start | bytes 393220
  337.7 32.0 %copy-start = (f32[3072,256]{1,0:T(8,128)}, f32[3072,256]{1,0:T(8,128)S(1)}, u32[]{:S(2)}) copy-start(f32[3072,256]{1,0:T(8,128)S(1)} %convolution_add_fusion) | copy-start | bytes 9437188
  388.9 0.9 copy-start.10
  388.9 2.0 copy-start.17
  388.9 184.7 %reduce-scatter.2.cloned.1.call-start = ((), (), s32[]{:S(2)}) async-start(), calls=%async_computation.4 | async-start | bytes 7077888 | tf_op jit(solution)/shard_map/reduce_scatter | solution.py:75
  424.6 1.2 copy-start.8
  424.6 219.8 %all-reduce.16.cloned.1.call-start = ((), (), s32[]{:S(2)}) async-start(), calls=%async_computation.6 | async-start | bytes 1048576 | tf_op jit(solution)/shard_map/psum | solution.py:87
  428.5 0.7 copy-start.13
  470.4 1.9 copy-start.12
  509.1 3.0 copy-start.4
  514.5 164.3 %all-gather.2.cloned.1.call-start = ((), (), s32[]{:S(2)}) async-start(), calls=%async_computation.5 | async-start | bytes 7077888 | tf_op jit(solution)/shard_map/all_gather | solution.py:86
  579.7 61.2 %copy-start.6 = (f32[256,256]{1,0:T(8,128)}, f32[256,256]{1,0:T(8,128)S(1)}, u32[]{:S(2)}) copy-start(f32[256,256]{1,0:T(8,128)S(1)} %convolution_add_fusion.2) | copy-start | bytes 786436
  641.2 6.0 copy-start.5
  644.4 4.3 copy-start.9
  647.2 3.0 copy-start.3
  678.8 5.1 copy-start.1
  678.8 5.1 copy-start.2
  (2 other events, 1.3 us)
Sparse Core Ops, SparseCore 0:
  60.0 133.3 all-reduce.9
  197.4 68.5 all-reduce.11
  284.6 67.5 all-reduce.13
  389.1 120.0 all-reduce.17
  512.9 60.6 reduce-scatter.1
  576.6 55.6 all-reduce.15
  634.2 44.5 all-gather.1
where the time goes:
time: 807 us; the launch traced here: 798 us
  other arithmetic  237 us (29%)
  waiting for transfers between devices  233 us (29%)
  matrix products  167 us (21%)
  local copies, waits for them, and re-layouts  140 us (17%)
  between operations  19.9 us (2%)
    psum x1, waiting for transfers between devices, on_device(): small = lax.psum(small, ('row', 'col'))  130 us
    dot_general x6, matrix products, fast_matmul(): jnp.dot(left, right, precision=lax.Precision.HIGH, preferred_element_type...  109 us
    unnamed x40, local copies, waits for them, and re-layouts  108 us
    another operation x14, other arithmetic, general_inverse(): lower = jnp.linalg.cholesky(matmul(square, square.T))  72.6 us
    another operation x14, other arithmetic, inverse_factor(): lower = jnp.linalg.cholesky(gram)  69.4 us
    reduce_scatter x1, waiting for transfers between devices, on_device(): lax.psum_scatter(jnp.concatenate([fast_matmul(amat, vectors_t.T), fast_ma...  58.9 us
    dot_general x22, matrix products, matmul(): jnp.dot(left, right, precision=lax.Precision.HIGHEST, preferred_element_t...  42.6 us
    another operation x4, other arithmetic, general_inverse(): linv = jax.scipy.linalg.solve_triangular(lower, ident, lower=True)  41.8 us
  transfers between devices with their start and end apart: 7, of which 5 were waited for; matrix products, arithmetic and copies ran while one was open for 42% of the time, Pallas kernels for 0%

commit v1 on v0

--- a/solution.py
+++ b/solution.py
@@ -2,8 +2,13 @@
 import jax.numpy as jnp
 from jax import lax
 from jax.sharding import PartitionSpec as P
+from jax.lax import all_gather
 
 NB = 256
+
+
+def mark_the_pieces_all(patch, device_axis):
+    return jnp.sum(all_gather(patch, axis_name=device_axis), axis=0)
 
 
 def broadcast(array, axis, root):
@@ -58,7 +63,7 @@
             ),
         ]
     )
-    small = lax.psum(small, ("row", "col"))
+    small = mark_the_pieces_all(small, ("row", "col"))
     own_panel, own_strip, small = lax.optimization_barrier((own_panel, own_strip, small))
     panel = broadcast(own_panel, "col", 0)
     strip = broadcast(own_strip, "row", last_row)

time: 807 us -> 842 us (1.043)
  waiting for transfers between devices: 233 us -> 297 us
  local copies, waits for them, and re-layouts: 140 us -> 98 us
  other arithmetic: 237 us -> 248 us
    all_gather x0 -> x1, waiting for transfers between devices: none -> 195 us  [mark_the_pieces_all(): return jnp.sum(all_gather(patch, axis_name=device_axis), axis=0)]
    psum x1 -> x0, waiting for transfers between devices: 130 us -> none  [on_device(): small = lax.psum(small, ('row', 'col'))]
    unnamed x40 -> x38, local copies, waits for them, and re-layouts: 108 us -> 65.7 us
    reduce_sum x0 -> x1, other arithmetic: none -> 12.9 us  [mark_the_pieces_all(): return jnp.sum(all_gather(patch, axis_name=device_axis), axis=0)]
  transfers between devices with their start and end apart: 7 -> 7, of which waited for: 5 -> 5; matrix products, arithmetic and copies ran while one was open for 42% -> 40% of each run, Pallas kernels for 0% -> 0%
where the time goes in v1:
time: 842 us; the launch traced here: 833 us
  waiting for transfers between devices  297 us (35%)
  other arithmetic  248 us (29%)
  matrix products  168 us (20%)
  local copies, waits for them, and re-layouts  98 us (12%)
  between operations  19.9 us (2%)
    all_gather x1, waiting for transfers between devices, mark_the_pieces_all(): return jnp.sum(all_gather(patch, axis_name=device_axis), axis=0)  195 us
    dot_general x6, matrix products, fast_matmul(): jnp.dot(left, right, precision=lax.Precision.HIGH, preferred_element_type...  112 us
    another operation x14, other arithmetic, general_inverse(): lower = jnp.linalg.cholesky(matmul(square, square.T))  72.6 us
    another operation x14, other arithmetic, inverse_factor(): lower = jnp.linalg.cholesky(gram)  69.4 us
    unnamed x38, local copies, waits for them, and re-layouts  65.7 us
    reduce_scatter x1, waiting for transfers between devices, on_device(): lax.psum_scatter(jnp.concatenate([fast_matmul(amat, vectors_t.T), fast_ma...  58.9 us
    another operation x4, other arithmetic, general_inverse(): linv = jax.scipy.linalg.solve_triangular(lower, ident, lower=True)  41.8 us
    dot_general x22, matrix products, matmul(): jnp.dot(left, right, precision=lax.Precision.HIGHEST, preferred_element_t...  41.4 us
  transfers between devices with their start and end apart: 7, of which 5 were waited for; matrix products, arithmetic and copies ran while one was open for 40% of the time, Pallas kernels for 0%

profile of v1, /device:TPU:0, one launch (start us, length us, event | category | flops | bytes accessed | tf_op | source)
XLA Modules:
  0.0 833.1 jit_solution(17811043873348135209)
XLA Ops:
  11.3 16.4 %copy.47 = f32[1,3072,1,1536]{3,1,2,0:T(8,128)} copy(f32[1,3072,1,1536]{3,2,1,0:T(1,128)} %param.5) | data formatting | bytes 37748736
  40.1 194.8 %all-gather.6.cloned.1.call-done = f32[128,256,256]{2,1,0:T(8,128)} async-done(((f32[4,256,256]{2,1,0:T(8,128)}), f32[128,256,256]{2,1,0:T(8,128)}) %all-gather.6.cloned.1.call-update) | async-done | bytes 33554448 | tf_op jit(solution)/shard_map/all_gather | solution.py:11
  234.9 12.9 %reduce_sum.9 = f32[4,256,256]{2,1,0:T(8,128)} reduce(f32[32,4,256,256]{3,2,1,0:T(8,128)} %bitcast.207, f32[]{:T(128)} %constant.74.clone.1), dimensions={0}, to_apply=%region_0.1 | reduce | flops 8126464 | bytes 34603012 | tf_op jit(solution)/shard_map/reduce_sum | solution.py:11
  267.4 11.7 %cholesky.214 = f32[128,128]{1,0:T(8,128)S(1)} custom-call(f32[128,128]{1,0:T(8,128)S(1)} %cholesky.346), custom_call_target="Cholesky" | custom-call | tf_op jit(solution)/shard_map/jit(cholesky)/cholesky | solution.py:24
  302.5 11.7 %cholesky.265 = f32[128,128]{1,0:T(8,128)S(1)} custom-call(f32[128,128]{1,0:T(8,128)S(1)} %convolution_subtract_fusion.8), custom_call_target="Cholesky" | custom-call | tf_op jit(solution)/shard_map/jit(cholesky)/cholesky | solution.py:24
  317.1 11.7 %cholesky.231 = f32[128,128]{1,0:T(8,128)S(1)} custom-call(f32[128,128]{1,0:T(8,128)S(1)} %convolution_subtract_fusion.9), custom_call_target="Cholesky" | custom-call | tf_op jit(solution)/shard_map/jit(cholesky)/cholesky | solution.py:24
  341.4 19.7 %custom-call.20 = f32[2,128,128]{1,2,0:T(8,128)S(1)} custom-call(f32[2,128,128]{2,1,0:T(8,128)S(1)} %get-tuple-element.39), custom_call_target="InvertDiagBlocksLowerTriangular" | custom-call | tf_op jit(solution)/shard_map/jit(_solve_triangular)/triangular_solve | solution.py:26
  361.1 19.7 %custom-call.18 = f32[2,128,128]{1,2,0:T(8,128)S(1)} custom-call(f32[2,128,128]{2,1,0:T(8,128)S(1)} %get-tuple-element.38), custom_call_target="InvertDiagBlocksLowerTriangular" | custom-call | tf_op jit(solution)/shard_map/jit(_solve_triangular)/triangular_solve | solution.py:26
  387.9 16.8 %all-reduce.11.cloned.1.call-done = f32[256,1536]{1,0:T(8,128)} async-done(((f32[256,1536]{1,0:T(8,128)}), f32[256,1536]{1,0:T(8,128)}) %all-reduce.11.cloned.1.call-update) | async-done | bytes 1572880 | tf_op jit(solution)/shard_map/psum | solution.py:16
  404.7 17.5 %fusion = f32[256,1536]{1,0:T(8,128)} fusion(f32[3072,256]{1,0:T(8,128)S(1)} %convolution_add_fusion, f32[1,3072,1,1536]{3,2,1,0:T(1,128)} %param.6), kind=kOutput, calls=%fused_computation.9 | convolution fusion | flops 7247757312 | bytes 23592960 | tf_op jit(solution)/shard_map/dot_general | solution.py:37
  422.1 17.3 %fusion.80 = f32[256,1536]{1,0:T(8,128)} fusion(f32[3072,256]{1,0:T(8,128)S(1)} %convolution_add_fusion, f32[1,3072,1,1536]{3,2,1,0:T(1,128)} %param.5), kind=kOutput, calls=%fused_computation.172 | convolution fusion | flops 7247757312 | bytes 23592960 | tf_op jit(solution)/shard_map/dot_general | solution.py:37
  444.7 15.4 %fusion.9 = f32[3072,256]{0,1:T(8,128)S(1)} fusion(f32[256,1536]{1,0:T(8,128)S(1)} %convolution_add_fusion.1, f32[1,3072,1,1536]{3,2,1,0:T(1,128)} %param.6), kind=kOutput, calls=%fused_computation.23 | convolution fusion | flops 7247757312 | bytes 23592960 | tf_op jit(solution)/shard_map/dot_general | solution.py:37
  460.1 15.3 %convolution_bitcast_fusion = f32[3072,256]{0,1:T(8,128)S(1)} fusion(f32[256,1536]{1,0:T(8,128)S(1)} %convolution_add_fusion.1, f32[1,3072,1,1536]{3,2,1,0:T(1,128)} %param.5), kind=kOutput, calls=%fused_computation.24 | convolution fusion | flops 7247757312 | bytes 23592960 | tf_op jit(solution)/shard_map/dot_general | solution.py:37
  509.8 13.2 %cholesky.299 = f32[128,128]{1,0:T(8,128)} custom-call(f32[128,128]{1,0:T(8,128)} %convolution_subtract_fusion.7), custom_call_target="Cholesky" | custom-call | tf_op jit(solution)/shard_map/jit(cholesky)/cholesky | solution.py:30
  533.6 21.1 %custom-call.22 = f32[2,128,128]{1,2,0:T(8,128)} custom-call(f32[2,128,128]{2,1,0:T(8,128)} %get-tuple-element.40), custom_call_target="InvertDiagBlocksLowerTriangular" | custom-call | tf_op jit(solution)/shard_map/jit(_solve_triangular)/triangular_solve | solution.py:32
  565.4 58.9 %reduce-scatter.2.cloned.1.call-done = f32[384,512]{0,1:T(8,128)} async-done(((f32[3072,512]{0,1:T(8,128)}), f32[384,512]{0,1:T(8,128)}) %reduce-scatter.2.cloned.1.call-update) | async-done | bytes 786448 | tf_op jit(solution)/shard_map/reduce_scatter | solution.py:80
  630.9 11.7 %cholesky.316 = f32[128,128]{1,0:T(8,128)S(1)} custom-call(f32[128,128]{1,0:T(8,128)S(1)} %cholesky.355), custom_call_target="Cholesky" | custom-call | tf_op jit(solution)/shard_map/jit(cholesky)/cholesky | solution.py:30
  653.0 12.1 %cholesky.333 = f32[128,128]{1,0:T(8,128)S(1)} custom-call(f32[128,128]{1,0:T(8,128)S(1)} %convolution_subtract_fusion.6), custom_call_target="Cholesky" | custom-call | tf_op jit(solution)/shard_map/jit(cholesky)/cholesky | solution.py:30
  671.7 19.7 %custom-call.24 = f32[2,128,128]{1,2,0:T(8,128)S(1)} custom-call(f32[2,128,128]{2,1,0:T(8,128)S(1)} %get-tuple-element.41), custom_call_target="InvertDiagBlocksLowerTriangular" | custom-call | tf_op jit(solution)/shard_map/jit(_solve_triangular)/triangular_solve | solution.py:32
  704.8 25.2 %all-gather.4.cloned.1.call-done = f32[3072,512]{1,0:T(8,128)} async-done(((f32[384,512]{1,0:T(8,128)}), f32[3072,512]{1,0:T(8,128)}) %all-gather.4.cloned.1.call-update) | async-done | bytes 6291472 | tf_op jit(solution)/shard_map/all_gather | solution.py:91
  735.2 23.6 %fusion.4 = f32[1,3072,1,1536]{3,1,2,0:T(8,128)} fusion(f32[1,3072,1,1536]{3,2,1,0:T(1,128)} %param.6, f32[3072,256]{1,0:T(8,128)S(1)} %copy-done.1, f32[3072,256]{1,0:T(8,128)} %get-tuple-element.88, f32[256,1536]{1,0:T(8,128)S(1)} %convolution_add_fusion.1, f32[256,1536]{1,0:T(8,128)S(1)} %copy-done.6), kind=kOutput, calls=%fused_computation.13 | convolution fusion | flops 14502592512 | bytes 47185920 | tf_op jit(solution)/shard_map/dot_general | solution.py:37
  758.8 22.3 %copy.23 = f32[1,3072,1,1536]{3,2,1,0:T(1,128)} copy(f32[1,3072,1,1536]{3,1,2,0:T(8,128)} %fusion.4) | data formatting | bytes 37748736
  781.0 22.8 %subtract_bitcast_fusion = f32[1,3072,1,1536]{3,1,2,0:T(8,128)} fusion(f32[3072,256]{1,0:T(8,128)S(1)} %copy-done.1, f32[3072,256]{1,0:T(8,128)S(1)} %get-tuple-element.89, f32[256,1536]{1,0:T(8,128)S(1)} %convolution_add_fusion.1, f32[256,1536]{1,0:T(8,128)S(1)} %fusion.92, f32[1,3072,1,1536]{3,2,1,0:T(1,128)} %param.5), kind=kOutput, calls=%fused_computation.15 | convolution fusion | flops 14502592512 | bytes 47185920 | tf_op jit(solution)/shard_map/dot_general | solution.py:37
  803.8 22.3 %copy.22 = f32[1,3072,1,1536]{3,2,1,0:T(1,128)} copy(f32[1,3072,1,1536]{3,1,2,0:T(8,128)} %subtract_bitcast_fusion) | data formatting | bytes 37748736
  (182 shorter events, 196.2 us)
Async XLA Ops:
  7.2 227.7 %all-gather.6.cloned.1.call-start = ((), (), s32[]{:S(2)}) async-start(), calls=%async_computation.6 | async-start | bytes 34603008 | tf_op jit(solution)/shard_map/all_gather | solution.py:11
  9.8 25.9 %copy-start.2 = (f32[1,256,1,1536]{3,1,2,0:T(8,128)}, f32[1,256,1,1536]{3,1,2,0:T(8,128)S(1)}, u32[]{:S(2)}) copy-start(f32[1,256,1,1536]{3,1,2,0:T(8,128)S(1)} %copy.48) | copy-start | bytes 4718596
  37.9 345.5 %all-reduce.9.cloned.1.call-start = ((), (), s32[]{:S(2)}) async-start(), calls=%async_computation.1 | async-start | bytes 6291456 | tf_op jit(solution)/shard_map/psum | solution.py:16
  249.7 1.2 copy-start.4
  249.7 155.0 %all-reduce.11.cloned.1.call-start = ((), (), s32[]{:S(2)}) async-start(), calls=%async_computation.2 | async-start | bytes 3145728 | tf_op jit(solution)/shard_map/psum | solution.py:16
  252.0 79.9 %copy-start.3 = (f32[1,256,1,1536]{3,1,2,0:T(8,128)S(1)}, f32[1,256,1,1536]{3,1,2,0:T(8,128)}, u32[]{:S(2)}) copy-start(f32[1,256,1,1536]{3,1,2,0:T(8,128)} %copy-done.2) | copy-start | bytes 4718596
  254.1 0.7 copy-start.13
  337.1 46.3 %copy-start.10 = (f32[256,256]{1,0:T(8,128)}, f32[256,256]{1,0:T(8,128)S(1)}, u32[]{:S(2)}) copy-start(f32[256,256]{1,0:T(8,128)S(1)} %get-tuple-element.327) | copy-start | bytes 786436
  337.1 222.8 %all-reduce.15.cloned.1.call-start = ((), (), s32[]{:S(2)}) async-start(), calls=%async_computation.7 | async-start | bytes 6291456 | tf_op jit(solution)/shard_map/psum | solution.py:77
  361.1 20.7 %copy-start.15 = (f32[2,128,128]{1,2,0:T(8,128)}, f32[2,128,128]{1,2,0:T(8,128)S(1)}, u32[]{:S(2)}) copy-start(f32[2,128,128]{1,2,0:T(8,128)S(1)} %custom-call.20) | copy-start | bytes 393220
  387.9 34.2 %copy-start = (f32[3072,256]{1,0:T(8,128)}, f32[3072,256]{1,0:T(8,128)S(1)}, u32[]{:S(2)}) copy-start(f32[3072,256]{1,0:T(8,128)S(1)} %convolution_add_fusion) | copy-start | bytes 9437188
  439.4 0.9 copy-start.9
  439.4 2.0 copy-start.16
  439.5 184.9 %reduce-scatter.2.cloned.1.call-start = ((), (), s32[]{:S(2)}) async-start(), calls=%async_computation.3 | async-start | bytes 7077888 | tf_op jit(solution)/shard_map/reduce_scatter | solution.py:80
  478.5 1.3 copy-start.5
  478.5 214.9 %all-reduce.13.cloned.1.call-start = ((), (), s32[]{:S(2)}) async-start(), calls=%async_computation.5 | async-start | bytes 1048576 | tf_op jit(solution)/shard_map/psum | solution.py:92
  482.6 0.7 copy-start.12
  495.0 0.6 copy-start.14
  524.5 2.0 copy-start.11
  559.8 3.0 copy-start.8
  565.2 164.9 %all-gather.4.cloned.1.call-start = ((), (), s32[]{:S(2)}) async-start(), calls=%async_computation.4 | async-start | bytes 7077888 | tf_op jit(solution)/shard_map/all_gather | solution.py:91
  696.2 5.7 copy-start.7
  730.1 5.1 copy-start.1
  730.1 5.1 copy-start.6
Sparse Core Ops, SparseCore 0:
  38.0 196.8 all-gather.5
  249.8 67.8 all-reduce.8
  337.2 67.4 all-reduce.10
  439.6 120.2 all-reduce.14
  563.6 60.6 reduce-scatter.1
  627.3 55.6 all-reduce.12
  685.5 44.5 all-gather.3
